TPU v7x, 32 devices: a 4x4x1 block of a 4x4x8 slice. The times are simulated.
32 devices in a mesh: rep: 2 (over z, core), dp: 16 (over x, y).
Axes of the slice: x: 4, y: 4, z: 1, core: 2. Of those that a mesh axis runs over, the one named last changes fastest.
The devices are a block of a 4x4x8 slice.
Arguments:
- g_w_gate: bfloat16 [32, 2, 768, 3072], P(('rep', 'dp')), parts along dimension 0
- g_w_up: bfloat16 [32, 2, 768, 3072], P(('rep', 'dp')), parts along dimension 0
- g_w_down: bfloat16 [32, 2, 3072, 768], P(('rep', 'dp')), parts along dimension 0
- w_gate: bfloat16 [2, 768, 3072], replicated
- w_up: bfloat16 [2, 768, 3072], replicated
- w_down: bfloat16 [2, 3072, 768], replicated
- m_w_gate: float32 [2, 768, 3072], P(None, 'dp')
- m_w_up: float32 [2, 768, 3072], P(None, 'dp')
- m_w_down: float32 [2, 3072, 768], P(None, 'dp')
- v_w_gate: float32 [2, 768, 3072], P(None, 'dp')
- v_w_up: float32 [2, 768, 3072], P(None, 'dp')
- v_w_down: float32 [2, 3072, 768], P(None, 'dp')
Outputs:
- output 1: bfloat16 [4, 768, 3072], P('rep'), parts along dimension 0
- output 2: bfloat16 [4, 768, 3072], P('rep'), parts along dimension 0
- output 3: bfloat16 [4, 3072, 768], P('rep'), parts along dimension 0
- output 4: float32 [4, 768, 3072], P('rep', 'dp'), parts along dimension 0
- output 5: float32 [4, 768, 3072], P('rep', 'dp'), parts along dimension 0
- output 6: float32 [4, 3072, 768], P('rep', 'dp'), parts along dimension 0
- output 7: float32 [4, 768, 3072], P('rep', 'dp'), parts along dimension 0
- output 8: float32 [4, 768, 3072], P('rep', 'dp'), parts along dimension 0
- output 9: float32 [4, 3072, 768], P('rep', 'dp'), parts along dimension 0
There are 2 independent parts. A program takes and returns all parts, laid end to end along the dimension named above; an argument that names none is the same for every part.
All inputs are finite; a program needn't handle non-finite values.
Results may differ from a plain program's by a relative error of at most 0.022.
Values are sent between devices in bfloat16 or wider.
A program may use at most 768 MiB of HBM per device.

v0:
```python
import jax
import jax.numpy as jnp
from jax import lax
from jax.sharding import PartitionSpec as P


def adamw(w, m, v, g):
    m = 0.9 * m + 0.1 * g
    v = 0.95 * v + 0.05 * g * g
    step = m * lax.rsqrt(v + 1e-8) + 0.1 * w
    return (w - 0.02 * step).astype(jnp.bfloat16), m, v


def clipped(gradients, sum_of_squares, count):
    factor = jnp.minimum(1.0, 0.5 * lax.rsqrt(sum_of_squares / count + 1e-30))
    return [g * factor for g in gradients]


def solution(mesh):
    def step(*arrays):
        terms, weights, m, v = (arrays[i : i + 3] for i in (0, 3, 6, 9))
        gradients = [lax.psum_scatter(t[0], "dp", scatter_dimension=1, tiled=True).astype(jnp.float32) for t in terms]
        squares = lax.psum(sum(jnp.sum(g * g) for g in gradients), "dp")
        gradients = clipped(gradients, squares, lax.psum(1, "dp") * sum(g.size for g in gradients))
        me = lax.axis_index("dp")
        own = [lax.dynamic_slice_in_dim(w, me * one.shape[1], one.shape[1], 1).astype(jnp.float32) for w, one in zip(weights, m, strict=True)]
        new = [adamw(w, m, v, g) for w, m, v, g in zip(own, m, v, gradients, strict=True)]
        whole = [lax.all_gather(one[0], "dp", axis=1, tiled=True) for one in new]
        return (*whole, *(one[1] for one in new), *(one[2] for one in new))

    all_of, cut = P(None, None, None), P(None, "dp", None)
    return jax.shard_map(
        step,
        mesh=mesh,
        in_specs=(P(("rep", "dp"), None, None, None),) * 3 + (all_of,) * 3 + (cut,) * 6,
        out_specs=(P("rep", None, None),) * 3 + (P("rep", "dp", None),) * 6,
        check_vma=False,
    )
```

profile of v0, /device:TPU:97, one launch (start us, length us, event | category | flops | bytes accessed | tf_op | source)
XLA Modules:
  0.0 555.8 jit_solution(7041572799435840402)
XLA Ops:
  7.3 0.7 reduce-scatter.4.cloned.1.call-update
  8.0 0.1 reduce-scatter.6.cloned.1.call-start
  8.1 0.7 reduce-scatter.6.cloned.1.call-update
  8.8 0.1 reduce-scatter.8.cloned.1.call-start
  8.9 0.7 reduce-scatter.8.cloned.1.call-update
  9.6 0.1 all-gather.8.cloned.1.call-start
  9.7 86.5 %reduce-scatter.4.cloned.1.call-done = bf16[2,48,3072]{2,1,0:T(8,128)(2,1)} async-done(((bf16[2,768,3072]{2,1,0:T(8,128)(2,1)}), bf16[2,48,3072]{2,1,0:T(8,128)(2,1)}) %reduce-scatter.4.cloned.1.call-update) | async-done | bytes 589840 | tf_op jit(solution)/shard_map/reduce_scatter | solution.py:22
  96.2 2.0 fusion.9
  98.1 83.2 %reduce-scatter.6.cloned.1.call-done = bf16[2,48,3072]{2,1,0:T(8,128)(2,1)} async-done(((bf16[2,768,3072]{2,1,0:T(8,128)(2,1)}), bf16[2,48,3072]{2,1,0:T(8,128)(2,1)}) %reduce-scatter.6.cloned.1.call-update) | async-done | bytes 589840 | tf_op jit(solution)/shard_map/reduce_scatter | solution.py:22
  181.3 2.0 fusion.10
  184.6 81.9 %reduce-scatter.8.cloned.1.call-done = bf16[2,192,768]{2,1,0:T(8,128)(2,1)} async-done(((bf16[2,3072,768]{2,1,0:T(8,128)(2,1)}), bf16[2,192,768]{2,1,0:T(8,128)(2,1)}) %reduce-scatter.8.cloned.1.call-update) | async-done | bytes 589840 | tf_op jit(solution)/shard_map/reduce_scatter | solution.py:22
  266.4 2.0 fusion.11
  269.1 31.4 %psum.7 = f32[]{:T(128)} all-reduce(f32[]{:T(128)S(6)} %add.65), channel_id=1, replica_groups=mesh['rep'=2,'dp'=16] {'dp'}, use_global_device_ids=true, to_apply=%region_6.0 | all-reduce | flops 1 | bytes 8 | tf_op jit(solution)/shard_map/psum | solution.py:23
  301.2 3.2 fusion.17
  304.5 0.1 all-gather.4.cloned.1.call-start
  304.6 3.9 fusion.8
  308.5 0.1 all-gather.6.cloned.1.call-start
  308.6 3.0 fusion.14
  311.7 67.7 %all-gather.8.cloned.1.call-done = bf16[2,3072,768]{2,1,0:T(8,128)(2,1)} async-done(((bf16[2,192,768]{2,1,0:T(8,128)(2,1)}), bf16[2,3072,768]{2,1,0:T(8,128)(2,1)}) %all-gather.8.cloned.1.call-update) | async-done | bytes 9437200 | tf_op jit(solution)/shard_map/all_gather | solution.py:28
  379.4 72.4 %all-gather.4.cloned.1.call-done = bf16[2,768,3072]{2,1,0:T(8,128)(2,1)} async-done(((bf16[2,48,3072]{2,1,0:T(8,128)(2,1)}), bf16[2,768,3072]{2,1,0:T(8,128)(2,1)}) %all-gather.4.cloned.1.call-update) | async-done | bytes 9437200 | tf_op jit(solution)/shard_map/all_gather | solution.py:28
  451.8 72.4 %all-gather.6.cloned.1.call-done = bf16[2,768,3072]{2,1,0:T(8,128)(2,1)} async-done(((bf16[2,48,3072]{2,1,0:T(8,128)(2,1)}), bf16[2,768,3072]{2,1,0:T(8,128)(2,1)}) %all-gather.6.cloned.1.call-update) | async-done | bytes 9437200 | tf_op jit(solution)/shard_map/all_gather | solution.py:28
  524.3 8.3 %copy.24 = bf16[2,768,3072]{2,1,0:T(8,128)(2,1)} copy(bf16[2,768,3072]{2,1,0:T(8,128)(2,1)} %all-gather.4.cloned.1.call-done) | data formatting | bytes 18874368
  532.5 8.3 %copy.25 = bf16[2,768,3072]{2,1,0:T(8,128)(2,1)} copy(bf16[2,768,3072]{2,1,0:T(8,128)(2,1)} %all-gather.6.cloned.1.call-done) | data formatting | bytes 18874368
  540.9 8.0 %copy.26 = bf16[2,3072,768]{2,1,0:T(8,128)(2,1)} copy(bf16[2,3072,768]{2,1,0:T(8,128)(2,1)} %all-gather.8.cloned.1.call-done) | data formatting | bytes 18874368
  (16 shorter events, 0.3 us)
Async XLA Ops:
  7.2 89.0 %reduce-scatter.4.cloned.1.call-start = ((), (), s32[]{:S(2)}) async-start(), calls=%async_computation.3 | async-start | bytes 10027008 | tf_op jit(solution)/shard_map/reduce_scatter | solution.py:22
  8.0 173.3 %reduce-scatter.6.cloned.1.call-start = ((), (), s32[]{:S(2)}) async-start(), calls=%async_computation.4 | async-start | bytes 10027008 | tf_op jit(solution)/shard_map/reduce_scatter | solution.py:22
  8.8 257.6 %reduce-scatter.8.cloned.1.call-start = ((), (), s32[]{:S(2)}) async-start(), calls=%async_computation.5 | async-start | bytes 10027008 | tf_op jit(solution)/shard_map/reduce_scatter | solution.py:22
  8.9 292.3 %copy-start.3 = (f32[2,192,768]{2,1,0:T(8,128)S(1)}, f32[2,192,768]{2,1,0:T(8,128)}, u32[]{:S(2)}) copy-start(f32[2,192,768]{2,1,0:T(8,128)} %param.20) | copy-start | bytes 3538948
  9.6 291.6 %copy-start.2 = (f32[2,192,768]{2,1,0:T(8,128)S(1)}, f32[2,192,768]{2,1,0:T(8,128)}, u32[]{:S(2)}) copy-start(f32[2,192,768]{2,1,0:T(8,128)} %param.23) | copy-start | bytes 3538948
  9.6 369.8 %all-gather.8.cloned.1.call-start = ((), (), s32[]{:S(2)}) async-start(), calls=%async_computation.8 | async-start | bytes 10027008 | tf_op jit(solution)/shard_map/all_gather | solution.py:28
  301.2 3.4 copy-start.1
  304.5 147.4 %all-gather.4.cloned.1.call-start = ((), (), s32[]{:S(2)}) async-start(), calls=%async_computation.6 | async-start | bytes 10027008 | tf_op jit(solution)/shard_map/all_gather | solution.py:28
  304.5 4.0 copy-start
  304.6 4.0 copy-start.4
  304.6 4.0 copy-start.5
  308.5 215.7 %all-gather.6.cloned.1.call-start = ((), (), s32[]{:S(2)}) async-start(), calls=%async_computation.7 | async-start | bytes 10027008 | tf_op jit(solution)/shard_map/all_gather | solution.py:28
Sparse Core Ops, SparseCore 0:
  11.3 84.7 reduce-scatter.3
  99.5 81.7 reduce-scatter.5
  184.6 81.7 reduce-scatter.7
  304.6 74.7 all-gather.7
  381.8 69.9 all-gather.3
  454.2 69.9 all-gather.5
where the time goes:
time: 556 us
  waiting for transfers between devices  466 us (84%)
  blocking collectives  31.4 us (6%)
  local copies, waits for them, and re-layouts  24.7 us (4%)
  between operations  16.9 us (3%)
  other arithmetic  16 us (3%)
    reduce_scatter x3, waiting for transfers between devices, step(): lax.psum_scatter(t[0], 'dp', scatter_dimension=1, tiled=True)  252 us
    all_gather x3, waiting for transfers between devices, step(): whole = [lax.all_gather(one[0], 'dp', axis=1, tiled=True) for one in new]  213 us
    psum x1, blocking collectives, step(): squares = lax.psum(sum((jnp.sum(g * g) for g in gradients)), 'dp')  31.4 us
    unnamed x15, local copies, waits for them, and re-layouts  24.7 us
  transfers between devices with their start and end apart: 6, of which 6 were waited for; matrix products, arithmetic and copies ran while one was open for 2% of the time, Pallas kernels for 0%

commit v1 on v0

v1 whole, which is shorter than its diff:
```python
import functools
import heapq
import math

import jax
import jax.numpy as jnp
from jax import lax
from jax.experimental import pallas as pl
from jax.experimental.pallas import tpu as pltpu
from jax.sharding import PartitionSpec as P

MESH = pl.DeviceIdType.MESH
F32 = jnp.float32
PARTS = (0, 1)
HALVES = (0, 1)
RINGS = 5
SLAB_SENDS = 6


def gather_sends(part, ring):
    axis = 1 - part if ring == 0 else part
    return [(0, 1, 0, axis), (1, -1, 1, axis), (2, 1, 1, axis), (3, -1, 0, axis), (4, 1, 0, axis), (5, -1, 1, axis)]


def gather_next(arrays_and_parts):
    follow = {}
    for a, p in arrays_and_parts:
        for kind, k, half in ((0, 3, 0), (1, 1, 1), (2, 3, 1), (3, 1, 0), (4, 2, 0), (5, 2, 1)):
            relay = [(a, p, 0, 4 + kind)] if kind < 2 else []
            follow[a, p, 0, kind] = relay + [(a, p, 1 + k, 0 if half == 0 else 1), (a, p, 1 + k, 3 if half == 0 else 2)]
        for k in range(4):
            for kind in range(SLAB_SENDS):
                follow[a, p, 1 + k, kind] = [(a, p, 1 + k, 4 + kind)] if kind < 2 else []
    free = {}
    arrivals = []
    order = []

    def put(send, now):
        a, p, ring, kind = send
        _, direction, _, axis = gather_sends(p, ring)[kind]
        start = max(now, free.get((axis, direction), 0.0))
        free[axis, direction] = start + 3.2
        heapq.heappush(arrivals, (start + 3.2 + 2.0, len(order) + len(arrivals), send))

    for i, (a, p) in enumerate(arrays_and_parts):
        for ring in (0, 1):
            for kind in range(4):
                put((a, p, ring, kind), 0.4 * i)
    while arrivals:
        now, _, send = heapq.heappop(arrivals)
        order.append((send, follow[send]))
        for one in follow[send]:
            put(one, now)
    return order


def kernel(side, count, *refs):
    terms, weights, m_in, v_in, whole, m_out, v_out = (refs[3 * i : 3 * i + 3] for i in range(7))
    own, weight = refs[21:24], refs[24:27]
    squares, load_sem, send_sem, recv_sem, gsend_sem, grecv_sem, nsend_sem, nrecv_sem = refs[27:]
    arrays = range(3)
    me = lax.axis_index("dp")
    at = (me // side, me % side)

    def device(axis, by):
        moved = lax.rem(at[axis] + by + side, side)
        return {"dp": moved * side + at[1] if axis == 0 else at[0] * side + moved}

    def place(axis, by):
        return lax.rem(at[axis] + by + side, side)

    def columns(a, half):
        wide = terms[a].shape[-1] // 2
        return pl.ds(half * wide, wide)

    def row_blocks(a):
        rows = terms[a].shape[-2]
        return 3 if rows % 48 == 0 else 1

    def load(a, p, which):
        if which == 0:
            t = place(p, 0)
            source = terms[a].at[0, p, t] if p == 0 else terms[a].at[0, p, :, t]
            return pltpu.make_async_copy(source, own[a].at[p, 0], load_sem.at[a, p, 0])
        half = which - 1
        t = place(p, 1 if half == 0 else -1)
        cols = columns(a, half)
        source = terms[a].at[0, p, t, :, :, cols] if p == 0 else terms[a].at[0, p, :, t, :, cols]
        return pltpu.make_async_copy(source, own[a].at[p, 1, :, :, cols], load_sem.at[a, p, which])

    def load_state(a, which):
        if which == 0:
            return pltpu.make_async_copy(weights[a].at[:, at[0], at[1]], weight[a], load_sem.at[a, 0, 3])
        if which == 1:
            return pltpu.make_async_copy(m_in[a], m_out[a], load_sem.at[a, 1, 3])
        return pltpu.make_async_copy(v_in[a], v_out[a], load_sem.at[a, 0, 4])

    for a in arrays:
        for p in PARTS:
            for half in HALVES:
                load(a, p, 1 + half).start()

    barrier = pltpu.get_barrier_semaphore()
    for by in range(1, side * side):
        pl.semaphore_signal(barrier, inc=1, device_id={"dp": lax.rem(me + by, side * side)}, device_id_type=MESH)
    pl.semaphore_wait(barrier, side * side - 1)

    def first(a, p, half, kind):
        up = 1 if half == 0 else -1
        cols = columns(a, half)
        if kind == 2:
            source, by = own[a].at[p, 1, :, :, cols], up
        else:
            by = up if kind == 0 else -up
            t = place(p, 2 if kind == 0 else by)
            source = terms[a].at[0, p, t, :, :, cols] if p == 0 else terms[a].at[0, p, :, t, :, cols]
        return pltpu.make_async_remote_copy(
            src_ref=source,
            dst_ref=whole[a].at[p, kind, :, :, cols],
            send_sem=send_sem.at[a, p, half, kind],
            recv_sem=recv_sem.at[a, p, half, kind],
            device_id=device(p, by),
            device_id_type=MESH,
        )

    def second(a, p, half, kind):
        up = 1 if half == 0 else -1
        cols = columns(a, half)
        by = -up if kind == 1 else up
        j = place(1 - p, 2 if kind == 0 else by)
        return pltpu.make_async_remote_copy(
            src_ref=own[a].at[p, 0, j, :, cols],
            dst_ref=whole[a].at[p, 3, kind, :, cols],
            send_sem=send_sem.at[a, p, half, 3 + kind],
            recv_sem=recv_sem.at[a, p, half, 3 + kind],
            device_id=device(1 - p, by),
            device_id_type=MESH,
        )

    def rows_of(a, i):
        rows = terms[a].shape[-2] // row_blocks(a)
        return pl.ds(pl.multiple_of(i * rows, rows), rows)

    def add(a, p, half, j, extra):
        cols = columns(a, half)

        def body(i, carry):
            rows = rows_of(a, i)
            total = own[a][p, 0, j, rows, cols].astype(F32)
            for k in (1, 2):
                total += whole[a][p, k, j, rows, cols].astype(F32)
            for k in extra:
                total += whole[a][p, 3, k, rows, cols].astype(F32)
            total = total.astype(jnp.bfloat16)
            own[a][p, 0, j, rows, cols] = total
            if carry is None:
                return None
            total = total.astype(F32)
            total = total * total
            total = sum(total[:, c : c + 128] for c in range(0, total.shape[1], 128))
            return carry + sum(total[r : r + 8] for r in range(0, total.shape[0], 8))

        return body

    every = [(p, half) for p in PARTS for half in HALVES]
    for a in arrays:
        for p, half in every:
            first(a, p, half, 0).start()
    for a in arrays:
        for p in PARTS:
            load(a, p, 0).start()
    for a in arrays:
        for which in range(3):
            load_state(a, which).start()
    for a in arrays:
        for p, half in every:
            first(a, p, half, 1).start()
            load(a, p, 1 + half).wait()
            first(a, p, half, 0).wait_recv()
            cols = columns(a, half)
            blocks = row_blocks(a)

            def relay(i, _, a=a, p=p, cols=cols, blocks=blocks):
                j, rows = i // blocks, rows_of(a, i % blocks)
                total = own[a][p, 1, j, rows, cols].astype(F32) + whole[a][p, 0, j, rows, cols].astype(F32)
                own[a][p, 1, j, rows, cols] = total.astype(jnp.bfloat16)

            lax.fori_loop(0, side * blocks, relay, None)
            first(a, p, half, 2).start()
    for a in arrays:
        for p in PARTS:
            load(a, p, 0).wait()
        for p, half in every:
            up = 1 if half == 0 else -1
            first(a, p, half, 1).wait_recv()
            first(a, p, half, 2).wait_recv()
            for kind in (0, 1):
                j = place(1 - p, 2 if kind == 0 else -up)
                lax.fori_loop(0, row_blocks(a), lambda i, c, f=add(a, p, half, j, ()): f(i, c), None)
                second(a, p, half, kind).start()
    for a in arrays:
        for p, half in every:
            up = 1 if half == 0 else -1
            second(a, p, half, 0).wait_recv()
            lax.fori_loop(0, row_blocks(a), lambda i, c, f=add(a, p, half, place(1 - p, up), (0,)): f(i, c), None)
            second(a, p, half, 2).start()
    total = jnp.zeros((8, 128), F32)
    for a in arrays:
        for p, half in every:
            second(a, p, half, 1).wait_recv()
            second(a, p, half, 2).wait_recv()
            total = lax.fori_loop(0, row_blocks(a), add(a, p, half, at[1 - p], (1, 2)), total)

    squares[me] = total

    def tell(by):
        return pltpu.make_async_remote_copy(
            src_ref=squares.at[me],
            dst_ref=squares.at[me],
            send_sem=nsend_sem.at[by - 1],
            recv_sem=nrecv_sem.at[by - 1],
            device_id={"dp": lax.rem(me + by, side * side)},
            device_id_type=MESH,
        )

    for by in range(1, side * side):
        tell(by).start()
    for a in arrays:
        for which in range(3):
            load_state(a, which).wait()
        for p, half in every:
            for kind in range(3):
                first(a, p, half, kind).wait_send()
                second(a, p, half, kind).wait_send()
    for by in range(1, side * side):
        tell(by).wait_recv()
    total = squares[0]
    for i in range(1, side * side):
        total += squares[i]
    total = jnp.sum(jnp.sum(total, axis=1, keepdims=True), axis=0, keepdims=True)
    factor = jnp.minimum(1.0, 0.5 * lax.rsqrt(total / count + 1e-30))

    def send(a, p, ring, kind):
        _, direction, half, axis = gather_sends(p, ring)[kind]
        cols = columns(a, half)
        back = direction if kind >= 4 else 0
        along = place(axis, -back)
        if ring == 0:
            other = at[1 - axis]
        else:
            other = place(1 - axis, ring - 1)
        block = whole[a].at[p, along, other, :, cols] if axis == 0 else whole[a].at[p, other, along, :, cols]
        return pltpu.make_async_remote_copy(
            src_ref=block,
            dst_ref=block,
            send_sem=gsend_sem.at[a, p, ring, kind],
            recv_sem=grecv_sem.at[a, p, ring, kind],
            device_id=device(axis, direction),
            device_id_type=MESH,
        )

    slabs = [(a, p) for a in arrays for p in PARTS]
    for a, p in slabs:
        for half in HALVES:
            cols = columns(a, half)

            def update(i, _, a=a, p=p, cols=cols):
                rows = rows_of(a, i)
                g = own[a][p, 0, at[1 - p], rows, cols].astype(F32) * factor
                w = weight[a][p, rows, cols].astype(F32)
                m = 0.9 * m_out[a][p, rows, cols] + 0.1 * g
                v = 0.95 * v_out[a][p, rows, cols] + 0.05 * g * g
                m_out[a][p, rows, cols] = m
                v_out[a][p, rows, cols] = v
                step = m * lax.rsqrt(v + 1e-8) + 0.1 * w
                whole[a][p, at[0], at[1], rows, cols] = (w - 0.02 * step).astype(jnp.bfloat16)

            lax.fori_loop(0, row_blocks(a), update, None)
        for ring in (0, 1):
            for kind in range(4):
                send(a, p, ring, kind).start()
    for one, then in gather_next(slabs):
        send(*one).wait_recv()
        for other in then:
            send(*other).start()
    for a, p in slabs:
        for ring in range(RINGS):
            for kind in range(SLAB_SENDS):
                send(a, p, ring, kind).wait_send()
    for by in range(1, side * side):
        tell(by).wait_send()


def store(*refs):
    here, there, sem = refs[:9], refs[9:18], refs[18]
    copies = [pltpu.make_async_copy(a, b, sem.at[i]) for i, (a, b) in enumerate(zip(here, there, strict=True))]
    for copy in copies:
        copy.start()
    for copy in copies:
        copy.wait()


def solution(mesh):
    devices = mesh.shape["dp"]
    side = math.isqrt(devices)

    def step(*arrays):
        terms, weights, m, v = (arrays[i : i + 3] for i in (0, 3, 6, 9))

        def blocks(x):
            return x.reshape(*x.shape[:-2], side, side, x.shape[-2] // devices, x.shape[-1])

        shapes = [one.shape for one in m]
        wholes = [blocks(w).shape for w in weights]
        count = devices * sum(math.prod(s) for s in shapes)
        out = pl.pallas_call(
            functools.partial(kernel, side, count),
            out_shape=[pltpu.VMEM(s, jnp.bfloat16) for s in wholes] + [pltpu.VMEM(s, F32) for s in shapes * 2],
            in_specs=[pl.BlockSpec(memory_space=pltpu.HBM)] * 12,
            out_specs=[pl.BlockSpec(memory_space=pltpu.VMEM)] * 9,
            scratch_shapes=[pltpu.VMEM((2, 2, side, *s[1:]), jnp.bfloat16) for s in shapes]
            + [pltpu.VMEM(s, jnp.bfloat16) for s in shapes]
            + [
                pltpu.VMEM((devices, 8, 128), F32),
                pltpu.SemaphoreType.DMA((3, 2, 5)),
                pltpu.SemaphoreType.DMA((3, 2, 2, 6)),
                pltpu.SemaphoreType.DMA((3, 2, 2, 6)),
                pltpu.SemaphoreType.DMA((3, 2, RINGS, SLAB_SENDS)),
                pltpu.SemaphoreType.DMA((3, 2, RINGS, SLAB_SENDS)),
                pltpu.SemaphoreType.DMA((devices - 1,)),
                pltpu.SemaphoreType.DMA((devices - 1,)),
            ],
            compiler_params=pltpu.CompilerParams(collective_id=0, has_side_effects=True, vmem_limit_bytes=20 * 2**20),
        )(*(blocks(t) for t in terms), *(blocks(w) for w in weights), *m, *v)
        out = pl.pallas_call(
            store,
            out_shape=[jax.ShapeDtypeStruct(o.shape, o.dtype) for o in out],
            in_specs=[pl.BlockSpec(memory_space=pltpu.VMEM)] * 9,
            out_specs=[pl.BlockSpec(memory_space=pltpu.HBM)] * 9,
            scratch_shapes=[pltpu.SemaphoreType.DMA((9,))],
            compiler_params=pltpu.CompilerParams(vmem_limit_bytes=2**20),
        )(*(pltpu.with_memory_space_constraint(o, pltpu.VMEM) for o in out))
        return (*(o.reshape(w.shape) for o, w in zip(out[:3], weights, strict=True)), *out[3:])

    all_of, cut = P(None, None, None), P(None, "dp", None)
    return jax.shard_map(
        step,
        mesh=mesh,
        in_specs=(P(("rep", "dp"), None, None, None),) * 3 + (all_of,) * 3 + (cut,) * 6,
        out_specs=(P("rep", None, None),) * 3 + (P("rep", "dp", None),) * 6,
        check_vma=False,
    )
```

time: 556 us -> 325 us (0.58)
  waiting for transfers between devices: 466 us -> 0 us
  Pallas kernels: 0 us -> 316 us
  blocking collectives: 31.4 us -> 0 us
  local copies, waits for them, and re-layouts: 24.7 us -> 7.42 us
  between operations: 16.9 us -> 0.66 us
  other arithmetic: 16 us -> 0 us
    pallas_call x0 -> x2, Pallas kernels: none -> 316 us  [the longest x1 304 us: step(): pl.pallas_call(functools.partial(kernel, side, count), out_shape=[pltpu.V...]
    reduce_scatter x3 -> x0, waiting for transfers between devices: 252 us -> none  [step(): lax.psum_scatter(t[0], 'dp', scatter_dimension=1, tiled=True)]
    all_gather x3 -> x0, waiting for transfers between devices: 213 us -> none  [step(): whole = [lax.all_gather(one[0], 'dp', axis=1, tiled=True) for one in new]]
    psum x1 -> x0, blocking collectives: 31.4 us -> none  [step(): squares = lax.psum(sum((jnp.sum(g * g) for g in gradients)), 'dp')]
    unnamed x15 -> x4, local copies, waits for them, and re-layouts: 24.7 us -> 7.42 us
    convert_element_type x3 -> x0, other arithmetic: 10.1 us -> none  [adamw(): return ((w - 0.02 * step).astype(jnp.bfloat16), m, v)]
    reduce_sum x3 -> x0, other arithmetic: 5.92 us -> none  [step(): squares = lax.psum(sum((jnp.sum(g * g) for g in gradients)), 'dp')]
  transfers between devices with their start and end apart: 6 -> 0, of which waited for: 6 -> 0; matrix products, arithmetic and copies ran while one was open for 2% -> 0% of each run, Pallas kernels for 0% -> 0%
where the time goes in v1:
time: 325 us; the launch traced here: 324 us
  Pallas kernels  316 us (97%)
  local copies, waits for them, and re-layouts  7.42 us (2%)
    pallas_call x1, Pallas kernels, step(): pl.pallas_call(functools.partial(kernel, side, count), out_shape=[pltpu.V...  304 us
    pallas_call x1, Pallas kernels, step(): pl.pallas_call(store, out_shape=[jax.ShapeDtypeStruct(o.shape, o.dtype) f...  11.6 us
    unnamed x4, local copies, waits for them, and re-layouts  7.42 us

profile of v1, /device:TPU:97, one launch (start us, length us, event | category | flops | bytes accessed | tf_op | source)
XLA Modules:
  0.0 323.9 jit_solution(5479656788120257520)
XLA Ops:
  0.6 304.2 %shard_map.187 = (bf16[2,4,4,48,3072]{4,3,2,1,0:T(8,128)(2,1)S(1)}, bf16[2,4,4,48,3072]{4,3,2,1,0:T(8,128)(2,1)S(1)}, bf16[2,4,4,192,768]{4,3,2,1,0:T(8,128)(2,1...) custom-call(bf16[1,2,4,4,48,3072]{5,4,3,2,1,0:T(8,128)(2,1)} %bitcas, ...), custom_call_target="tpu_custom_call" | custom-call | tf_op jit(solution)/shard_map/pallas_call | solution.py:316
  304.8 0.0 copy-start
  304.8 3.7 %copy-done = bf16[2,4,4,48,3072]{4,3,2,1,0:T(8,128)(2,1)} copy-done((bf16[2,4,4,48,3072]{4,3,2,1,0:T(8,128)(2,1)}, bf16[2,4,4,48,3072]{4,3,2,1,0:T(8,128)(2,1)S(1)}, u32[]{:S(2)}) %copy-start) | copy-done | bytes 9437208
  308.6 0.0 copy-start.1
  308.6 3.7 %copy-done.1 = bf16[2,4,4,48,3072]{4,3,2,1,0:T(8,128)(2,1)S(1)} copy-done((bf16[2,4,4,48,3072]{4,3,2,1,0:T(8,128)(2,1)S(1)}, bf16[2,4,4,48,3072]{4,3,2,1,0:T(8,128)(2,1)}, u32[]{:S(2)}) %copy-start.1) | copy-done | bytes 9437208
  312.2 11.6 %shard_map.188 = (bf16[2,4,4,48,3072]{4,3,2,1,0:T(8,128)(2,1)}, bf16[2,4,4,48,3072]{4,3,2,1,0:T(8,128)(2,1)}, bf16[2,4,4,192,768]{4,3,2,1,0:T(8,128)(2,1)}, f32[...) custom-call(bf16[2,4,4,48,3072]{4,3,2,1,0:T(8,128)(2,1)S(1)} %get-tu, ...), custom_call_target="tpu_custom_call" | custom-call | tf_op jit(solution)/shard_map/pallas_call | solution.py:335
Async XLA Ops:
  304.8 3.7 %copy-start = (bf16[2,4,4,48,3072]{4,3,2,1,0:T(8,128)(2,1)}, bf16[2,4,4,48,3072]{4,3,2,1,0:T(8,128)(2,1)S(1)}, u32[]{:S(2)}) copy-start(bf16[2,4,4,48,3072]{4,3,2,1,0:T(8,128)(2,1)S(1)} %get-tuple-element.28.refs_1_) | copy-start | bytes 28311556
  308.6 3.7 %copy-start.1 = (bf16[2,4,4,48,3072]{4,3,2,1,0:T(8,128)(2,1)S(1)}, bf16[2,4,4,48,3072]{4,3,2,1,0:T(8,128)(2,1)}, u32[]{:S(2)}) copy-start(bf16[2,4,4,48,3072]{4,3,2,1,0:T(8,128)(2,1)} %copy-done) | copy-start | bytes 28311556

commit v2 on v1

--- a/solution.py
+++ b/solution.py
@@ -14,37 +14,40 @@
 PARTS = (0, 1)
 HALVES = (0, 1)
 RINGS = 5
-SLAB_SENDS = 6
-
-
-def gather_sends(part, ring):
-    axis = 1 - part if ring == 0 else part
-    return [(0, 1, 0, axis), (1, -1, 1, axis), (2, 1, 1, axis), (3, -1, 0, axis), (4, 1, 0, axis), (5, -1, 1, axis)]
-
-
-def gather_next(arrays_and_parts):
+KINDS = 6
+
+
+def gather_kinds(ring):
+    relays = {4: (1, 0, True), 5: (-1, 1, True)}
+    if ring == 3:
+        return {0: (1, 0, False), 1: (-1, 1, False), 2: (1, 1, False), 3: (-1, 0, False), **relays}
+    return {0: (1, None, False), 1: (-1, None, False), **relays}
+
+
+def gather_order(slabs):
     follow = {}
-    for a, p in arrays_and_parts:
-        for kind, k, half in ((0, 3, 0), (1, 1, 1), (2, 3, 1), (3, 1, 0), (4, 2, 0), (5, 2, 1)):
-            relay = [(a, p, 0, 4 + kind)] if kind < 2 else []
-            follow[a, p, 0, kind] = relay + [(a, p, 1 + k, 0 if half == 0 else 1), (a, p, 1 + k, 3 if half == 0 else 2)]
-        for k in range(4):
-            for kind in range(SLAB_SENDS):
-                follow[a, p, 1 + k, kind] = [(a, p, 1 + k, 4 + kind)] if kind < 2 else []
-    free = {}
-    arrivals = []
-    order = []
+    for a, p in slabs:
+        for ring in range(RINGS):
+            for kind, (_, _, relayed) in gather_kinds(ring).items():
+                follow[a, p, ring, kind] = [(a, p, ring, 4 + kind)] if kind < 2 else []
+        for kind, k in ((0, 3), (1, 1)):
+            follow[a, p, 0, kind] += [(a, p, 1 + k, 0), (a, p, 1 + k, 1)]
+        follow[a, p, 0, 4] += [(a, p, 3, 0), (a, p, 3, 3)]
+        follow[a, p, 0, 5] += [(a, p, 3, 1), (a, p, 3, 2)]
+    free, arrivals, order, made = {}, [], [], 0
 
     def put(send, now):
+        nonlocal made
         a, p, ring, kind = send
-        _, direction, _, axis = gather_sends(p, ring)[kind]
-        start = max(now, free.get((axis, direction), 0.0))
-        free[axis, direction] = start + 3.2
-        heapq.heappush(arrivals, (start + 3.2 + 2.0, len(order) + len(arrivals), send))
-
-    for i, (a, p) in enumerate(arrays_and_parts):
+        direction, half, _ = gather_kinds(ring)[kind]
+        way = (1 - p if ring == 0 else p, direction)
+        free[way] = max(now, free.get(way, 0.0)) + (6.4 if half is None else 3.2)
+        made += 1
+        heapq.heappush(arrivals, (free[way] + 2.0, made, send))
+
+    for i, (a, p) in enumerate(slabs):
         for ring in (0, 1):
-            for kind in range(4):
+            for kind in (0, 1):
                 put((a, p, ring, kind), 0.4 * i)
     while arrivals:
         now, _, send = heapq.heappop(arrivals)
@@ -101,9 +104,10 @@
                 load(a, p, 1 + half).start()
 
     barrier = pltpu.get_barrier_semaphore()
-    for by in range(1, side * side):
-        pl.semaphore_signal(barrier, inc=1, device_id={"dp": lax.rem(me + by, side * side)}, device_id_type=MESH)
-    pl.semaphore_wait(barrier, side * side - 1)
+    for axis in (0, 1):
+        for by in (1, -1):
+            pl.semaphore_signal(barrier, inc=1, device_id=device(axis, by), device_id_type=MESH)
+    pl.semaphore_wait(barrier, 4)
 
     def first(a, p, half, kind):
         up = 1 if half == 0 else -1
@@ -241,15 +245,13 @@
     factor = jnp.minimum(1.0, 0.5 * lax.rsqrt(total / count + 1e-30))
 
     def send(a, p, ring, kind):
-        _, direction, half, axis = gather_sends(p, ring)[kind]
-        cols = columns(a, half)
-        back = direction if kind >= 4 else 0
-        along = place(axis, -back)
-        if ring == 0:
-            other = at[1 - axis]
-        else:
-            other = place(1 - axis, ring - 1)
-        block = whole[a].at[p, along, other, :, cols] if axis == 0 else whole[a].at[p, other, along, :, cols]
+        direction, half, relayed = gather_kinds(ring)[kind]
+        axis = 1 - p if ring == 0 else p
+        along = place(axis, -direction if relayed else 0)
+        other = at[1 - axis] if ring == 0 else place(1 - axis, ring - 1)
+        block = whole[a].at[p, along, other] if axis == 0 else whole[a].at[p, other, along]
+        if half is not None:
+            block = block.at[:, columns(a, half)]
         return pltpu.make_async_remote_copy(
             src_ref=block,
             dst_ref=block,
@@ -277,15 +279,15 @@
 
             lax.fori_loop(0, row_blocks(a), update, None)
         for ring in (0, 1):
-            for kind in range(4):
+            for kind in (0, 1):
                 send(a, p, ring, kind).start()
-    for one, then in gather_next(slabs):
+    for one, then in gather_order(slabs):
         send(*one).wait_recv()
         for other in then:
             send(*other).start()
     for a, p in slabs:
         for ring in range(RINGS):
-            for kind in range(SLAB_SENDS):
+            for kind in gather_kinds(ring):
                 send(a, p, ring, kind).wait_send()
     for by in range(1, side * side):
         tell(by).wait_send()
@@ -325,8 +327,8 @@
                 pltpu.SemaphoreType.DMA((3, 2, 5)),
                 pltpu.SemaphoreType.DMA((3, 2, 2, 6)),
                 pltpu.SemaphoreType.DMA((3, 2, 2, 6)),
-                pltpu.SemaphoreType.DMA((3, 2, RINGS, SLAB_SENDS)),
-                pltpu.SemaphoreType.DMA((3, 2, RINGS, SLAB_SENDS)),
+                pltpu.SemaphoreType.DMA((3, 2, RINGS, KINDS)),
+                pltpu.SemaphoreType.DMA((3, 2, RINGS, KINDS)),
                 pltpu.SemaphoreType.DMA((devices - 1,)),
                 pltpu.SemaphoreType.DMA((devices - 1,)),
             ],
@@ -338,7 +340,7 @@
             in_specs=[pl.BlockSpec(memory_space=pltpu.VMEM)] * 9,
             out_specs=[pl.BlockSpec(memory_space=pltpu.HBM)] * 9,
             scratch_shapes=[pltpu.SemaphoreType.DMA((9,))],
-            compiler_params=pltpu.CompilerParams(vmem_limit_bytes=2**20),
+            compiler_params=pltpu.CompilerParams(vmem_limit_bytes=20 * 2**20),
         )(*(pltpu.with_memory_space_constraint(o, pltpu.VMEM) for o in out))
         return (*(o.reshape(w.shape) for o, w in zip(out[:3], weights, strict=True)), *out[3:])
 

time: 325 us -> 316 us (0.972)
  local copies, waits for them, and re-layouts: 7.42 us -> 0 us
    unnamed x4 -> x0, local copies, waits for them, and re-layouts: 7.42 us -> none
where the time goes in v2:
time: 316 us; the launch traced here: 315 us
  Pallas kernels  315 us (100%)
    pallas_call x1, Pallas kernels, step(): pl.pallas_call(functools.partial(kernel, side, count), out_shape=[pltpu.V...  303 us
    pallas_call x1, Pallas kernels, step(): pl.pallas_call(store, out_shape=[jax.ShapeDtypeStruct(o.shape, o.dtype) f...  11.7 us

profile of v2, /device:TPU:97, one launch (start us, length us, event | category | flops | bytes accessed | tf_op | source)
XLA Modules:
  0.0 315.3 jit_solution(12612678091914764189)
XLA Ops:
  0.6 303.0 %shard_map.187 = (bf16[2,4,4,48,3072]{4,3,2,1,0:T(8,128)(2,1)S(1)}, bf16[2,4,4,48,3072]{4,3,2,1,0:T(8,128)(2,1)S(1)}, bf16[2,4,4,192,768]{4,3,2,1,0:T(8,128)(2,1...) custom-call(bf16[1,2,4,4,48,3072]{5,4,3,2,1,0:T(8,128)(2,1)} %bitcas, ...), custom_call_target="tpu_custom_call" | custom-call | tf_op jit(solution)/shard_map/pallas_call | solution.py:318
  303.7 11.7 %shard_map.188 = (bf16[2,4,4,48,3072]{4,3,2,1,0:T(8,128)(2,1)}, bf16[2,4,4,48,3072]{4,3,2,1,0:T(8,128)(2,1)}, bf16[2,4,4,192,768]{4,3,2,1,0:T(8,128)(2,1)}, f32[...) custom-call(bf16[2,4,4,48,3072]{4,3,2,1,0:T(8,128)(2,1)S(1)} %get-tu, ...), custom_call_target="tpu_custom_call" | custom-call | tf_op jit(solution)/shard_map/pallas_call | solution.py:337

commit v3 on v2

--- a/solution.py
+++ b/solution.py
@@ -11,6 +11,7 @@
 
 MESH = pl.DeviceIdType.MESH
 F32 = jnp.float32
+LEAD_NS = 15200
 PARTS = (0, 1)
 HALVES = (0, 1)
 RINGS = 5
@@ -108,6 +109,7 @@
         for by in (1, -1):
             pl.semaphore_signal(barrier, inc=1, device_id=device(axis, by), device_id_type=MESH)
     pl.semaphore_wait(barrier, 4)
+    pl.delay(lax.rem(lax.axis_index("rep"), 2) * LEAD_NS)
 
     def first(a, p, half, kind):
         up = 1 if half == 0 else -1

time: 316 us -> 313 us (level)
  no operation moved by 1% of the time
where the time goes in v3:
time: 313 us
  Pallas kernels  312 us (100%)
    pallas_call x1, Pallas kernels, step(): pl.pallas_call(functools.partial(kernel, side, count), out_shape=[pltpu.V...  301 us
    pallas_call x1, Pallas kernels, step(): pl.pallas_call(store, out_shape=[jax.ShapeDtypeStruct(o.shape, o.dtype) f...  11.7 us

profile of v3, /device:TPU:97, one launch (start us, length us, event | category | flops | bytes accessed | tf_op | source)
XLA Modules:
  0.0 312.9 jit_solution(1858745095405471656)
XLA Ops:
  0.6 300.6 %shard_map.187 = (bf16[2,4,4,48,3072]{4,3,2,1,0:T(8,128)(2,1)S(1)}, bf16[2,4,4,48,3072]{4,3,2,1,0:T(8,128)(2,1)S(1)}, bf16[2,4,4,192,768]{4,3,2,1,0:T(8,128)(2,1...) custom-call(bf16[1,2,4,4,48,3072]{5,4,3,2,1,0:T(8,128)(2,1)} %bitcas, ...), custom_call_target="tpu_custom_call" | custom-call | tf_op jit(solution)/shard_map/pallas_call | solution.py:320
  301.3 11.7 %shard_map.188 = (bf16[2,4,4,48,3072]{4,3,2,1,0:T(8,128)(2,1)}, bf16[2,4,4,48,3072]{4,3,2,1,0:T(8,128)(2,1)}, bf16[2,4,4,192,768]{4,3,2,1,0:T(8,128)(2,1)}, f32[...) custom-call(bf16[2,4,4,48,3072]{4,3,2,1,0:T(8,128)(2,1)S(1)} %get-tu, ...), custom_call_target="tpu_custom_call" | custom-call | tf_op jit(solution)/shard_map/pallas_call | solution.py:339

commit v4 on v3

--- a/solution.py
+++ b/solution.py
@@ -11,7 +11,8 @@
 
 MESH = pl.DeviceIdType.MESH
 F32 = jnp.float32
-LEAD_NS = 15200
+LEAD_NS = 25000
+VMEM = 27 * 2**20
 PARTS = (0, 1)
 HALVES = (0, 1)
 RINGS = 5
@@ -58,24 +59,60 @@
     return order
 
 
-def kernel(side, count, *refs):
-    terms, weights, m_in, v_in, whole, m_out, v_out = (refs[3 * i : 3 * i + 3] for i in range(7))
-    own, weight = refs[21:24], refs[24:27]
-    squares, load_sem, send_sem, recv_sem, gsend_sem, grecv_sem, nsend_sem, nrecv_sem = refs[27:]
+def moved(side, at, axis, by):
+    return lax.rem(at[axis] + by + side, side)
+
+
+def device(side, at, axis, by):
+    to = moved(side, at, axis, by)
+    return {"dp": to * side + at[1] if axis == 0 else at[0] * side + to}
+
+
+def columns(wide, half):
+    return pl.ds(half * (wide // 2), wide // 2)
+
+
+def meet(side, at):
+    barrier = pltpu.get_barrier_semaphore()
+    for axis in (0, 1):
+        for by in (1, -1):
+            pl.semaphore_signal(barrier, inc=1, device_id=device(side, at, axis, by), device_id_type=MESH)
+    pl.semaphore_wait(barrier, 4)
+
+
+def gather_copy(side, at, whole, sems, part, ring, kind, own=None):
+    direction, half, relayed = gather_kinds(ring)[kind]
+    axis = 1 - part if ring == 0 else part
+    along = moved(side, at, axis, -direction if relayed else 0)
+    other = at[1 - axis] if ring == 0 else moved(side, at, 1 - axis, ring - 1)
+    block = whole.at[part, along, other] if axis == 0 else whole.at[part, other, along]
+    if half is not None:
+        block = block.at[:, columns(whole.shape[-1], half)]
+    return pltpu.make_async_remote_copy(
+        src_ref=own.at[part] if own is not None and ring < 2 and not relayed else block,
+        dst_ref=block,
+        send_sem=sems[0].at[part, ring, kind],
+        recv_sem=sems[1].at[part, ring, kind],
+        device_id=device(side, at, axis, direction),
+        device_id_type=MESH,
+    )
+
+
+def sum_and_step(side, count, *refs):
+    terms, weights, m_in, v_in = (refs[3 * i : 3 * i + 3] for i in range(4))
+    fresh = refs[14]
+    m_out, v_out, own, weight = (refs[15 + 3 * i : 18 + 3 * i] for i in range(4))
+    slots = (*refs[12:14], refs[27])
+    squares, load_sem, send_sem, recv_sem, gsend_sem, grecv_sem, nsend_sem, nrecv_sem = refs[28:]
     arrays = range(3)
     me = lax.axis_index("dp")
     at = (me // side, me % side)
 
-    def device(axis, by):
-        moved = lax.rem(at[axis] + by + side, side)
-        return {"dp": moved * side + at[1] if axis == 0 else at[0] * side + moved}
-
     def place(axis, by):
-        return lax.rem(at[axis] + by + side, side)
-
-    def columns(a, half):
-        wide = terms[a].shape[-1] // 2
-        return pl.ds(half * wide, wide)
+        return moved(side, at, axis, by)
+
+    def half_of(a, half):
+        return columns(terms[a].shape[-1], half)
 
     def row_blocks(a):
         rows = terms[a].shape[-2]
@@ -88,7 +125,7 @@
             return pltpu.make_async_copy(source, own[a].at[p, 0], load_sem.at[a, p, 0])
         half = which - 1
         t = place(p, 1 if half == 0 else -1)
-        cols = columns(a, half)
+        cols = half_of(a, half)
         source = terms[a].at[0, p, t, :, :, cols] if p == 0 else terms[a].at[0, p, :, t, :, cols]
         return pltpu.make_async_copy(source, own[a].at[p, 1, :, :, cols], load_sem.at[a, p, which])
 
@@ -104,16 +141,12 @@
             for half in HALVES:
                 load(a, p, 1 + half).start()
 
-    barrier = pltpu.get_barrier_semaphore()
-    for axis in (0, 1):
-        for by in (1, -1):
-            pl.semaphore_signal(barrier, inc=1, device_id=device(axis, by), device_id_type=MESH)
-    pl.semaphore_wait(barrier, 4)
+    meet(side, at)
     pl.delay(lax.rem(lax.axis_index("rep"), 2) * LEAD_NS)
 
     def first(a, p, half, kind):
         up = 1 if half == 0 else -1
-        cols = columns(a, half)
+        cols = half_of(a, half)
         if kind == 2:
             source, by = own[a].at[p, 1, :, :, cols], up
         else:
@@ -122,24 +155,24 @@
             source = terms[a].at[0, p, t, :, :, cols] if p == 0 else terms[a].at[0, p, :, t, :, cols]
         return pltpu.make_async_remote_copy(
             src_ref=source,
-            dst_ref=whole[a].at[p, kind, :, :, cols],
+            dst_ref=slots[a].at[p, kind, :, :, cols],
             send_sem=send_sem.at[a, p, half, kind],
             recv_sem=recv_sem.at[a, p, half, kind],
-            device_id=device(p, by),
+            device_id=device(side, at, p, by),
             device_id_type=MESH,
         )
 
     def second(a, p, half, kind):
         up = 1 if half == 0 else -1
-        cols = columns(a, half)
+        cols = half_of(a, half)
         by = -up if kind == 1 else up
         j = place(1 - p, 2 if kind == 0 else by)
         return pltpu.make_async_remote_copy(
             src_ref=own[a].at[p, 0, j, :, cols],
-            dst_ref=whole[a].at[p, 3, kind, :, cols],
+            dst_ref=slots[a].at[p, 3, kind, :, cols],
             send_sem=send_sem.at[a, p, half, 3 + kind],
             recv_sem=recv_sem.at[a, p, half, 3 + kind],
-            device_id=device(1 - p, by),
+            device_id=device(side, at, 1 - p, by),
             device_id_type=MESH,
         )
 
@@ -148,15 +181,15 @@
         return pl.ds(pl.multiple_of(i * rows, rows), rows)
 
     def add(a, p, half, j, extra):
-        cols = columns(a, half)
+        cols = half_of(a, half)
 
         def body(i, carry):
             rows = rows_of(a, i)
             total = own[a][p, 0, j, rows, cols].astype(F32)
             for k in (1, 2):
-                total += whole[a][p, k, j, rows, cols].astype(F32)
+                total += slots[a][p, k, j, rows, cols].astype(F32)
             for k in extra:
-                total += whole[a][p, 3, k, rows, cols].astype(F32)
+                total += slots[a][p, 3, k, rows, cols].astype(F32)
             total = total.astype(jnp.bfloat16)
             own[a][p, 0, j, rows, cols] = total
             if carry is None:
@@ -183,12 +216,12 @@
             first(a, p, half, 1).start()
             load(a, p, 1 + half).wait()
             first(a, p, half, 0).wait_recv()
-            cols = columns(a, half)
+            cols = half_of(a, half)
             blocks = row_blocks(a)
 
             def relay(i, _, a=a, p=p, cols=cols, blocks=blocks):
                 j, rows = i // blocks, rows_of(a, i % blocks)
-                total = own[a][p, 1, j, rows, cols].astype(F32) + whole[a][p, 0, j, rows, cols].astype(F32)
+                total = own[a][p, 1, j, rows, cols].astype(F32) + slots[a][p, 0, j, rows, cols].astype(F32)
                 own[a][p, 1, j, rows, cols] = total.astype(jnp.bfloat16)
 
             lax.fori_loop(0, side * blocks, relay, None)
@@ -246,43 +279,35 @@
     total = jnp.sum(jnp.sum(total, axis=1, keepdims=True), axis=0, keepdims=True)
     factor = jnp.minimum(1.0, 0.5 * lax.rsqrt(total / count + 1e-30))
 
-    def send(a, p, ring, kind):
-        direction, half, relayed = gather_kinds(ring)[kind]
-        axis = 1 - p if ring == 0 else p
-        along = place(axis, -direction if relayed else 0)
-        other = at[1 - axis] if ring == 0 else place(1 - axis, ring - 1)
-        block = whole[a].at[p, along, other] if axis == 0 else whole[a].at[p, other, along]
-        if half is not None:
-            block = block.at[:, columns(a, half)]
-        return pltpu.make_async_remote_copy(
-            src_ref=block,
-            dst_ref=block,
-            send_sem=gsend_sem.at[a, p, ring, kind],
-            recv_sem=grecv_sem.at[a, p, ring, kind],
-            device_id=device(axis, direction),
-            device_id_type=MESH,
-        )
-
-    slabs = [(a, p) for a in arrays for p in PARTS]
-    for a, p in slabs:
-        for half in HALVES:
-            cols = columns(a, half)
-
-            def update(i, _, a=a, p=p, cols=cols):
-                rows = rows_of(a, i)
-                g = own[a][p, 0, at[1 - p], rows, cols].astype(F32) * factor
-                w = weight[a][p, rows, cols].astype(F32)
-                m = 0.9 * m_out[a][p, rows, cols] + 0.1 * g
-                v = 0.95 * v_out[a][p, rows, cols] + 0.05 * g * g
-                m_out[a][p, rows, cols] = m
-                v_out[a][p, rows, cols] = v
-                step = m * lax.rsqrt(v + 1e-8) + 0.1 * w
-                whole[a][p, at[0], at[1], rows, cols] = (w - 0.02 * step).astype(jnp.bfloat16)
-
-            lax.fori_loop(0, row_blocks(a), update, None)
-        for ring in (0, 1):
-            for kind in (0, 1):
-                send(a, p, ring, kind).start()
+    def send(a, *which):
+        return gather_copy(side, at, slots[a], (gsend_sem.at[a], grecv_sem.at[a]), *which)
+
+    for a in arrays:
+        for p in PARTS:
+            for half in HALVES:
+                cols = half_of(a, half)
+
+                def update(i, _, a=a, p=p, cols=cols):
+                    rows = rows_of(a, i)
+                    g = own[a][p, 0, at[1 - p], rows, cols].astype(F32) * factor
+                    w = weight[a][p, rows, cols].astype(F32)
+                    m = 0.9 * m_out[a][p, rows, cols] + 0.1 * g
+                    v = 0.95 * v_out[a][p, rows, cols] + 0.05 * g * g
+                    m_out[a][p, rows, cols] = m
+                    v_out[a][p, rows, cols] = v
+                    step = m * lax.rsqrt(v + 1e-8) + 0.1 * w
+                    w = (w - 0.02 * step).astype(jnp.bfloat16)
+                    if a == 2:
+                        fresh[p, rows, cols] = w
+                    else:
+                        slots[a][p, at[0], at[1], rows, cols] = w
+
+                lax.fori_loop(0, row_blocks(a), update, None)
+            if a < 2:
+                for ring in (0, 1):
+                    for kind in (0, 1):
+                        send(a, p, ring, kind).start()
+    slabs = [(a, p) for a in (0, 1) for p in PARTS]
     for one, then in gather_order(slabs):
         send(*one).wait_recv()
         for other in then:
@@ -295,13 +320,50 @@
         tell(by).wait_send()
 
 
-def store(*refs):
-    here, there, sem = refs[:9], refs[9:18], refs[18]
-    copies = [pltpu.make_async_copy(a, b, sem.at[i]) for i, (a, b) in enumerate(zip(here, there, strict=True))]
-    for copy in copies:
-        copy.start()
-    for copy in copies:
-        copy.wait()
+def gather_last(side, fresh, whole, send_sem, recv_sem, copy_sem):
+    me = lax.axis_index("dp")
+    at = (me // side, me % side)
+    keep = [pltpu.make_async_copy(fresh.at[p], whole.at[p, at[0], at[1]], copy_sem.at[p]) for p in PARTS]
+    for p in PARTS:
+        keep[p].start()
+    meet(side, at)
+
+    def send(_, *which):
+        return gather_copy(side, at, whole, (send_sem, recv_sem), *which, own=fresh)
+
+    slabs = [(0, p) for p in PARTS]
+    for a, p in slabs:
+        for ring in (0, 1):
+            for kind in (0, 1):
+                send(a, p, ring, kind).start()
+    for one, then in gather_order(slabs):
+        send(*one).wait_recv()
+        for other in then:
+            send(*other).start()
+    for p in PARTS:
+        keep[p].wait()
+        for ring in range(RINGS):
+            for kind in gather_kinds(ring):
+                send(0, p, ring, kind).wait_send()
+
+
+def store(arrays, vmem):
+    def body(*refs):
+        here, there, sem = refs[: len(arrays)], refs[len(arrays) : -1], refs[-1]
+        copies = [pltpu.make_async_copy(a, b, sem.at[i]) for i, (a, b) in enumerate(zip(here, there, strict=True))]
+        for copy in copies:
+            copy.start()
+        for copy in copies:
+            copy.wait()
+
+    return pl.pallas_call(
+        body,
+        out_shape=[pltpu.HBM(x.shape, x.dtype) for x in arrays],
+        in_specs=[pl.BlockSpec(memory_space=pltpu.VMEM)] * len(arrays),
+        out_specs=[pl.BlockSpec(memory_space=pltpu.HBM)] * len(arrays),
+        scratch_shapes=[pltpu.SemaphoreType.DMA((len(arrays),))],
+        compiler_params=pltpu.CompilerParams(vmem_limit_bytes=vmem),
+    )(*(pltpu.with_memory_space_constraint(x, pltpu.VMEM) for x in arrays))
 
 
 def solution(mesh):
@@ -314,37 +376,43 @@
         def blocks(x):
             return x.reshape(*x.shape[:-2], side, side, x.shape[-2] // devices, x.shape[-1])
 
+        def here(shape, dtype):
+            return pltpu.VMEM(shape, dtype)
+
         shapes = [one.shape for one in m]
         wholes = [blocks(w).shape for w in weights]
         count = devices * sum(math.prod(s) for s in shapes)
-        out = pl.pallas_call(
-            functools.partial(kernel, side, count),
-            out_shape=[pltpu.VMEM(s, jnp.bfloat16) for s in wholes] + [pltpu.VMEM(s, F32) for s in shapes * 2],
+        gather_sems = [pltpu.SemaphoreType.DMA((2, RINGS, KINDS))] * 2
+        new = pl.pallas_call(
+            functools.partial(sum_and_step, side, count),
+            out_shape=[here(s, jnp.bfloat16) for s in (*wholes[:2], shapes[2])] + [here(s, F32) for s in shapes * 2],
             in_specs=[pl.BlockSpec(memory_space=pltpu.HBM)] * 12,
             out_specs=[pl.BlockSpec(memory_space=pltpu.VMEM)] * 9,
             scratch_shapes=[pltpu.VMEM((2, 2, side, *s[1:]), jnp.bfloat16) for s in shapes]
-            + [pltpu.VMEM(s, jnp.bfloat16) for s in shapes]
+            + [pltpu.VMEM(s, jnp.bfloat16) for s in (*shapes, wholes[2])]
             + [
                 pltpu.VMEM((devices, 8, 128), F32),
                 pltpu.SemaphoreType.DMA((3, 2, 5)),
                 pltpu.SemaphoreType.DMA((3, 2, 2, 6)),
                 pltpu.SemaphoreType.DMA((3, 2, 2, 6)),
-                pltpu.SemaphoreType.DMA((3, 2, RINGS, KINDS)),
-                pltpu.SemaphoreType.DMA((3, 2, RINGS, KINDS)),
+                pltpu.SemaphoreType.DMA((2, 2, RINGS, KINDS)),
+                pltpu.SemaphoreType.DMA((2, 2, RINGS, KINDS)),
                 pltpu.SemaphoreType.DMA((devices - 1,)),
                 pltpu.SemaphoreType.DMA((devices - 1,)),
             ],
-            compiler_params=pltpu.CompilerParams(collective_id=0, has_side_effects=True, vmem_limit_bytes=20 * 2**20),
-        )(*(blocks(t) for t in terms), *(blocks(w) for w in weights), *m, *v)
-        out = pl.pallas_call(
-            store,
-            out_shape=[jax.ShapeDtypeStruct(o.shape, o.dtype) for o in out],
-            in_specs=[pl.BlockSpec(memory_space=pltpu.VMEM)] * 9,
-            out_specs=[pl.BlockSpec(memory_space=pltpu.HBM)] * 9,
-            scratch_shapes=[pltpu.SemaphoreType.DMA((9,))],
-            compiler_params=pltpu.CompilerParams(vmem_limit_bytes=20 * 2**20),
-        )(*(pltpu.with_memory_space_constraint(o, pltpu.VMEM) for o in out))
-        return (*(o.reshape(w.shape) for o, w in zip(out[:3], weights, strict=True)), *out[3:])
+            compiler_params=pltpu.CompilerParams(collective_id=0, has_side_effects=True, vmem_limit_bytes=VMEM),
+        )(*(pltpu.with_memory_space_constraint(x, pltpu.HBM) for x in (*map(blocks, terms), *map(blocks, weights), *m, *v)))
+        new = store(new, VMEM)
+        last = pl.pallas_call(
+            functools.partial(gather_last, side),
+            out_shape=here(wholes[2], jnp.bfloat16),
+            in_specs=[pl.BlockSpec(memory_space=pltpu.HBM)],
+            out_specs=pl.BlockSpec(memory_space=pltpu.VMEM),
+            scratch_shapes=[*gather_sems, pltpu.SemaphoreType.DMA((2,))],
+            compiler_params=pltpu.CompilerParams(collective_id=1, has_side_effects=True, vmem_limit_bytes=VMEM),
+        )(pltpu.with_memory_space_constraint(new[2], pltpu.HBM))
+        (last,) = store([last], VMEM)
+        return (*(o.reshape(w.shape) for o, w in zip((*new[:2], last), weights, strict=True)), *new[3:])
 
     all_of, cut = P(None, None, None), P(None, "dp", None)
     return jax.shard_map(

time: 313 us -> 303 us (0.968)
  Pallas kernels: 312 us -> 302 us
    pallas_call x2 -> x4, Pallas kernels: 312 us -> 302 us  [the longest x1 256 us: step(): pl.pallas_call(functools.partial(sum_and_step, side, count), out_shape=[h...]
where the time goes in v4:
time: 303 us
  Pallas kernels  302 us (100%)
    pallas_call x1, Pallas kernels, step(): pl.pallas_call(functools.partial(sum_and_step, side, count), out_shape=[h...  256 us
    pallas_call x1, Pallas kernels, step(): pl.pallas_call(functools.partial(gather_last, side), out_shape=here(whole...  33.2 us
    pallas_call x2, Pallas kernels, store(): pl.pallas_call(body, out_shape=[pltpu.HBM(x.shape, x.dtype) for x in arra...  12.7 us

profile of v4, /device:TPU:97, one launch (start us, length us, event | category | flops | bytes accessed | tf_op | source)
XLA Modules:
  0.0 303.0 jit_solution(11567610594472575976)
XLA Ops:
  0.6 256.3 %shard_map.187 = (bf16[2,4,4,48,3072]{4,3,2,1,0:T(8,128)(2,1)S(1)}, bf16[2,4,4,48,3072]{4,3,2,1,0:T(8,128)(2,1)S(1)}, bf16[2,192,768]{2,1,0:T(8,128)(2,1)S(1)}, ...) custom-call(bf16[1,2,4,4,48,3072]{5,4,3,2,1,0:T(8,128)(2,1)} %bitcas, ...), custom_call_target="tpu_custom_call" | custom-call | tf_op jit(solution)/shard_map/pallas_call | solution.py:386
  257.0 9.0 %shard_map.188 = (bf16[2,4,4,48,3072]{4,3,2,1,0:T(8,128)(2,1)}, bf16[2,4,4,48,3072]{4,3,2,1,0:T(8,128)(2,1)}, bf16[2,192,768]{2,1,0:T(8,128)(2,1)}, f32[2,48,307...) custom-call(bf16[2,4,4,48,3072]{4,3,2,1,0:T(8,128)(2,1)S(1)} %get-tu, ...), custom_call_target="tpu_custom_call" | custom-call | tf_op jit(solution)/shard_map/pallas_call | solution.py:359
  266.0 33.2 %shard_map.189.refs_0_ = bf16[2,4,4,192,768]{4,3,2,1,0:T(8,128)(2,1)S(1)} custom-call(bf16[2,192,768]{2,1,0:T(8,128)(2,1)} %get-tuple-element.38.fresh), custom_call_target="tpu_custom_call" | custom-call | tf_op jit(solution)/shard_map/pallas_call | solution.py:406
  299.2 3.8 %shard_map.190 = bf16[2,4,4,192,768]{4,3,2,1,0:T(8,128)(2,1)} custom-call(bf16[2,4,4,192,768]{4,3,2,1,0:T(8,128)(2,1)S(1)} %shard_map.189.refs_0_), custom_call_target="tpu_custom_call" | custom-call | tf_op jit(solution)/shard_map/pallas_call | solution.py:359

commit v5 on v4

--- a/solution.py
+++ b/solution.py
@@ -11,7 +11,7 @@
 
 MESH = pl.DeviceIdType.MESH
 F32 = jnp.float32
-LEAD_NS = 25000
+LEAD_NS = 23500
 VMEM = 27 * 2**20
 PARTS = (0, 1)
 HALVES = (0, 1)
@@ -19,42 +19,51 @@
 KINDS = 6
 
 
-def gather_kinds(ring):
+def gather_kinds(ring, fine):
     relays = {4: (1, 0, True), 5: (-1, 1, True)}
-    if ring == 3:
+    if fine and ring == 3:
         return {0: (1, 0, False), 1: (-1, 1, False), 2: (1, 1, False), 3: (-1, 0, False), **relays}
     return {0: (1, None, False), 1: (-1, None, False), **relays}
 
 
-def gather_order(slabs):
-    follow = {}
+def gather_order(slabs, fine):
+    follow, waits = {}, {}
     for a, p in slabs:
-        for ring in range(RINGS):
-            for kind, (_, _, relayed) in gather_kinds(ring).items():
+        for ring in range(RINGS if fine else 2):
+            for kind, (_, _, relayed) in gather_kinds(ring, fine).items():
                 follow[a, p, ring, kind] = [(a, p, ring, 4 + kind)] if kind < 2 else []
-        for kind, k in ((0, 3), (1, 1)):
-            follow[a, p, 0, kind] += [(a, p, 1 + k, 0), (a, p, 1 + k, 1)]
-        follow[a, p, 0, 4] += [(a, p, 3, 0), (a, p, 3, 3)]
-        follow[a, p, 0, 5] += [(a, p, 3, 1), (a, p, 3, 2)]
+        if fine:
+            for kind, k in ((0, 3), (1, 1)):
+                follow[a, p, 0, kind] += [(a, p, 1 + k, 0), (a, p, 1 + k, 1)]
+            follow[a, p, 0, 4] += [(a, p, 3, 0), (a, p, 3, 3)]
+            follow[a, p, 0, 5] += [(a, p, 3, 1), (a, p, 3, 2)]
+        else:
+            waits[a, p] = 4
     free, arrivals, order, made = {}, [], [], 0
 
     def put(send, now):
         nonlocal made
         a, p, ring, kind = send
-        direction, half, _ = gather_kinds(ring)[kind]
+        direction, half, _ = gather_kinds(ring, fine)[kind]
         way = (1 - p if ring == 0 else p, direction)
-        free[way] = max(now, free.get(way, 0.0)) + (6.4 if half is None else 3.2)
+        time = (6.4 if half is None else 3.2) * (1 if fine or ring == 0 else 4)
+        free[way] = max(now, free.get(way, 0.0)) + time
         made += 1
         heapq.heappush(arrivals, (free[way] + 2.0, made, send))
 
     for i, (a, p) in enumerate(slabs):
-        for ring in (0, 1):
+        for ring in (0, 1) if fine else (0,):
             for kind in (0, 1):
                 put((a, p, ring, kind), 0.4 * i)
     while arrivals:
         now, _, send = heapq.heappop(arrivals)
-        order.append((send, follow[send]))
-        for one in follow[send]:
+        then = list(follow[send])
+        if send[2] == 0 and not fine:
+            waits[send[:2]] -= 1
+            if waits[send[:2]] == 0:
+                then += [(*send[:2], 1, 0), (*send[:2], 1, 1)]
+        order.append((send, then))
+        for one in then:
             put(one, now)
     return order
 
@@ -80,14 +89,19 @@
     pl.semaphore_wait(barrier, 4)
 
 
-def gather_copy(side, at, whole, sems, part, ring, kind, own=None):
-    direction, half, relayed = gather_kinds(ring)[kind]
+def gather_copy(side, at, whole, sems, fine, part, ring, kind, own=None):
+    direction, half, relayed = gather_kinds(ring, fine)[kind]
     axis = 1 - part if ring == 0 else part
     along = moved(side, at, axis, -direction if relayed else 0)
-    other = at[1 - axis] if ring == 0 else moved(side, at, 1 - axis, ring - 1)
-    block = whole.at[part, along, other] if axis == 0 else whole.at[part, other, along]
-    if half is not None:
-        block = block.at[:, columns(whole.shape[-1], half)]
+    if ring == 1 and not fine:
+        block = whole.at[part, along] if axis == 0 else whole.at[part, :, along]
+        if half is not None:
+            block = block.at[:, :, columns(whole.shape[-1], half)]
+    else:
+        other = at[1 - axis] if ring == 0 else moved(side, at, 1 - axis, ring - 1)
+        block = whole.at[part, along, other] if axis == 0 else whole.at[part, other, along]
+        if half is not None:
+            block = block.at[:, columns(whole.shape[-1], half)]
     return pltpu.make_async_remote_copy(
         src_ref=own.at[part] if own is not None and ring < 2 and not relayed else block,
         dst_ref=block,
@@ -135,11 +149,6 @@
         if which == 1:
             return pltpu.make_async_copy(m_in[a], m_out[a], load_sem.at[a, 1, 3])
         return pltpu.make_async_copy(v_in[a], v_out[a], load_sem.at[a, 0, 4])
-
-    for a in arrays:
-        for p in PARTS:
-            for half in HALVES:
-                load(a, p, 1 + half).start()
 
     meet(side, at)
     pl.delay(lax.rem(lax.axis_index("rep"), 2) * LEAD_NS)
@@ -206,6 +215,9 @@
         for p, half in every:
             first(a, p, half, 0).start()
     for a in arrays:
+        for p, half in every:
+            load(a, p, 1 + half).start()
+    for a in arrays:
         for p in PARTS:
             load(a, p, 0).start()
     for a in arrays:
@@ -250,7 +262,7 @@
             second(a, p, half, 2).wait_recv()
             total = lax.fori_loop(0, row_blocks(a), add(a, p, half, at[1 - p], (1, 2)), total)
 
-    squares[me] = total
+    squares[me] = jnp.sum(total, axis=0, keepdims=True)
 
     def tell(by):
         return pltpu.make_async_remote_copy(
@@ -276,11 +288,11 @@
     total = squares[0]
     for i in range(1, side * side):
         total += squares[i]
-    total = jnp.sum(jnp.sum(total, axis=1, keepdims=True), axis=0, keepdims=True)
+    total = jnp.sum(total, axis=1, keepdims=True)
     factor = jnp.minimum(1.0, 0.5 * lax.rsqrt(total / count + 1e-30))
 
     def send(a, *which):
-        return gather_copy(side, at, slots[a], (gsend_sem.at[a], grecv_sem.at[a]), *which)
+        return gather_copy(side, at, slots[a], (gsend_sem.at[a], grecv_sem.at[a]), False, *which)
 
     for a in arrays:
         for p in PARTS:
@@ -304,17 +316,16 @@
 
                 lax.fori_loop(0, row_blocks(a), update, None)
             if a < 2:
-                for ring in (0, 1):
-                    for kind in (0, 1):
-                        send(a, p, ring, kind).start()
+                for kind in (0, 1):
+                    send(a, p, 0, kind).start()
     slabs = [(a, p) for a in (0, 1) for p in PARTS]
-    for one, then in gather_order(slabs):
+    for one, then in gather_order(slabs, False):
         send(*one).wait_recv()
         for other in then:
             send(*other).start()
     for a, p in slabs:
-        for ring in range(RINGS):
-            for kind in gather_kinds(ring):
+        for ring in (0, 1):
+            for kind in gather_kinds(ring, False):
                 send(a, p, ring, kind).wait_send()
     for by in range(1, side * side):
         tell(by).wait_send()
@@ -329,21 +340,21 @@
     meet(side, at)
 
     def send(_, *which):
-        return gather_copy(side, at, whole, (send_sem, recv_sem), *which, own=fresh)
+        return gather_copy(side, at, whole, (send_sem, recv_sem), True, *which, own=fresh)
 
     slabs = [(0, p) for p in PARTS]
     for a, p in slabs:
         for ring in (0, 1):
             for kind in (0, 1):
                 send(a, p, ring, kind).start()
-    for one, then in gather_order(slabs):
+    for one, then in gather_order(slabs, True):
         send(*one).wait_recv()
         for other in then:
             send(*other).start()
     for p in PARTS:
         keep[p].wait()
         for ring in range(RINGS):
-            for kind in gather_kinds(ring):
+            for kind in gather_kinds(ring, True):
                 send(0, p, ring, kind).wait_send()
 
 
@@ -391,12 +402,12 @@
             scratch_shapes=[pltpu.VMEM((2, 2, side, *s[1:]), jnp.bfloat16) for s in shapes]
             + [pltpu.VMEM(s, jnp.bfloat16) for s in (*shapes, wholes[2])]
             + [
-                pltpu.VMEM((devices, 8, 128), F32),
+                pltpu.VMEM((devices, 1, 128), F32),
                 pltpu.SemaphoreType.DMA((3, 2, 5)),
                 pltpu.SemaphoreType.DMA((3, 2, 2, 6)),
                 pltpu.SemaphoreType.DMA((3, 2, 2, 6)),
-                pltpu.SemaphoreType.DMA((2, 2, RINGS, KINDS)),
-                pltpu.SemaphoreType.DMA((2, 2, RINGS, KINDS)),
+                pltpu.SemaphoreType.DMA((2, 2, 2, KINDS)),
+                pltpu.SemaphoreType.DMA((2, 2, 2, KINDS)),
                 pltpu.SemaphoreType.DMA((devices - 1,)),
                 pltpu.SemaphoreType.DMA((devices - 1,)),
             ],

time: 303 us -> 303 us (level)
  no operation moved by 1% of the time
where the time goes in v5:
time: 303 us; the launch traced here: 302 us
  Pallas kernels  302 us (100%)
    pallas_call x1, Pallas kernels, step(): pl.pallas_call(functools.partial(sum_and_step, side, count), out_shape=[h...  254 us
    pallas_call x1, Pallas kernels, step(): pl.pallas_call(functools.partial(gather_last, side), out_shape=here(whole...  34.7 us
    pallas_call x2, Pallas kernels, store(): pl.pallas_call(body, out_shape=[pltpu.HBM(x.shape, x.dtype) for x in arra...  12.7 us

profile of v5, /device:TPU:97, one launch (start us, length us, event | category | flops | bytes accessed | tf_op | source)
XLA Modules:
  0.0 302.5 jit_solution(17298976903296015609)
XLA Ops:
  0.6 254.4 %shard_map.187 = (bf16[2,4,4,48,3072]{4,3,2,1,0:T(8,128)(2,1)S(1)}, bf16[2,4,4,48,3072]{4,3,2,1,0:T(8,128)(2,1)S(1)}, bf16[2,192,768]{2,1,0:T(8,128)(2,1)S(1)}, ...) custom-call(bf16[1,2,4,4,48,3072]{5,4,3,2,1,0:T(8,128)(2,1)} %bitcas, ...), custom_call_target="tpu_custom_call" | custom-call | tf_op jit(solution)/shard_map/pallas_call | solution.py:397
  255.0 9.0 %shard_map.188 = (bf16[2,4,4,48,3072]{4,3,2,1,0:T(8,128)(2,1)}, bf16[2,4,4,48,3072]{4,3,2,1,0:T(8,128)(2,1)}, bf16[2,192,768]{2,1,0:T(8,128)(2,1)}, f32[2,48,307...) custom-call(bf16[2,4,4,48,3072]{4,3,2,1,0:T(8,128)(2,1)S(1)} %get-tu, ...), custom_call_target="tpu_custom_call" | custom-call | tf_op jit(solution)/shard_map/pallas_call | solution.py:370
  264.0 34.7 %shard_map.189.refs_0_ = bf16[2,4,4,192,768]{4,3,2,1,0:T(8,128)(2,1)S(1)} custom-call(bf16[2,192,768]{2,1,0:T(8,128)(2,1)} %get-tuple-element.38.fresh), custom_call_target="tpu_custom_call" | custom-call | tf_op jit(solution)/shard_map/pallas_call | solution.py:417
  298.7 3.8 %shard_map.190 = bf16[2,4,4,192,768]{4,3,2,1,0:T(8,128)(2,1)} custom-call(bf16[2,4,4,192,768]{4,3,2,1,0:T(8,128)(2,1)S(1)} %shard_map.189.refs_0_), custom_call_target="tpu_custom_call" | custom-call | tf_op jit(solution)/shard_map/pallas_call | solution.py:370

commit v6 on v5

--- a/solution.py
+++ b/solution.py
@@ -262,20 +262,27 @@
             second(a, p, half, 2).wait_recv()
             total = lax.fori_loop(0, row_blocks(a), add(a, p, half, at[1 - p], (1, 2)), total)
 
-    squares[me] = jnp.sum(total, axis=0, keepdims=True)
-
-    def tell(by):
+    def tell(axis, by):
+        mine = squares.at[axis, at[axis]]
         return pltpu.make_async_remote_copy(
-            src_ref=squares.at[me],
-            dst_ref=squares.at[me],
-            send_sem=nsend_sem.at[by - 1],
-            recv_sem=nrecv_sem.at[by - 1],
-            device_id={"dp": lax.rem(me + by, side * side)},
+            src_ref=mine,
+            dst_ref=mine,
+            send_sem=nsend_sem.at[axis, by - 1],
+            recv_sem=nrecv_sem.at[axis, by - 1],
+            device_id=device(side, at, axis, by),
             device_id_type=MESH,
         )
 
-    for by in range(1, side * side):
-        tell(by).start()
+    total = jnp.sum(total, axis=0, keepdims=True)
+    for axis in (0, 1):
+        squares[axis, at[axis]] = total
+        for by in range(1, side):
+            tell(axis, by).start()
+        for by in range(1, side):
+            tell(axis, by).wait_recv()
+        total = squares[axis, 0]
+        for i in range(1, side):
+            total += squares[axis, i]
     for a in arrays:
         for which in range(3):
             load_state(a, which).wait()
@@ -283,11 +290,6 @@
             for kind in range(3):
                 first(a, p, half, kind).wait_send()
                 second(a, p, half, kind).wait_send()
-    for by in range(1, side * side):
-        tell(by).wait_recv()
-    total = squares[0]
-    for i in range(1, side * side):
-        total += squares[i]
     total = jnp.sum(total, axis=1, keepdims=True)
     factor = jnp.minimum(1.0, 0.5 * lax.rsqrt(total / count + 1e-30))
 
@@ -327,8 +329,9 @@
         for ring in (0, 1):
             for kind in gather_kinds(ring, False):
                 send(a, p, ring, kind).wait_send()
-    for by in range(1, side * side):
-        tell(by).wait_send()
+    for axis in (0, 1):
+        for by in range(1, side):
+            tell(axis, by).wait_send()
 
 
 def gather_last(side, fresh, whole, send_sem, recv_sem, copy_sem):
@@ -402,14 +405,14 @@
             scratch_shapes=[pltpu.VMEM((2, 2, side, *s[1:]), jnp.bfloat16) for s in shapes]
             + [pltpu.VMEM(s, jnp.bfloat16) for s in (*shapes, wholes[2])]
             + [
-                pltpu.VMEM((devices, 1, 128), F32),
+                pltpu.VMEM((2, side, 1, 128), F32),
                 pltpu.SemaphoreType.DMA((3, 2, 5)),
                 pltpu.SemaphoreType.DMA((3, 2, 2, 6)),
                 pltpu.SemaphoreType.DMA((3, 2, 2, 6)),
                 pltpu.SemaphoreType.DMA((2, 2, 2, KINDS)),
                 pltpu.SemaphoreType.DMA((2, 2, 2, KINDS)),
-                pltpu.SemaphoreType.DMA((devices - 1,)),
-                pltpu.SemaphoreType.DMA((devices - 1,)),
+                pltpu.SemaphoreType.DMA((2, side - 1)),
+                pltpu.SemaphoreType.DMA((2, side - 1)),
             ],
             compiler_params=pltpu.CompilerParams(collective_id=0, has_side_effects=True, vmem_limit_bytes=VMEM),
         )(*(pltpu.with_memory_space_constraint(x, pltpu.HBM) for x in (*map(blocks, terms), *map(blocks, weights), *m, *v)))

time: 303 us -> 302 us (level)
  no operation moved by 1% of the time
where the time goes in v6:
time: 302 us
  Pallas kernels  302 us (100%)
    pallas_call x1, Pallas kernels, step(): pl.pallas_call(functools.partial(sum_and_step, side, count), out_shape=[h...  254 us
    pallas_call x1, Pallas kernels, step(): pl.pallas_call(functools.partial(gather_last, side), out_shape=here(whole...  35.1 us
    pallas_call x2, Pallas kernels, store(): pl.pallas_call(body, out_shape=[pltpu.HBM(x.shape, x.dtype) for x in arra...  12.7 us

profile of v6, /device:TPU:97, one launch (start us, length us, event | category | flops | bytes accessed | tf_op | source)
XLA Modules:
  0.0 302.3 jit_solution(6300432636168119081)
XLA Ops:
  0.6 253.8 %shard_map.187 = (bf16[2,4,4,48,3072]{4,3,2,1,0:T(8,128)(2,1)S(1)}, bf16[2,4,4,48,3072]{4,3,2,1,0:T(8,128)(2,1)S(1)}, bf16[2,192,768]{2,1,0:T(8,128)(2,1)S(1)}, ...) custom-call(bf16[1,2,4,4,48,3072]{5,4,3,2,1,0:T(8,128)(2,1)} %bitcas, ...), custom_call_target="tpu_custom_call" | custom-call | tf_op jit(solution)/shard_map/pallas_call | solution.py:400
  254.4 9.0 %shard_map.188 = (bf16[2,4,4,48,3072]{4,3,2,1,0:T(8,128)(2,1)}, bf16[2,4,4,48,3072]{4,3,2,1,0:T(8,128)(2,1)}, bf16[2,192,768]{2,1,0:T(8,128)(2,1)}, f32[2,48,307...) custom-call(bf16[2,4,4,48,3072]{4,3,2,1,0:T(8,128)(2,1)S(1)} %get-tu, ...), custom_call_target="tpu_custom_call" | custom-call | tf_op jit(solution)/shard_map/pallas_call | solution.py:373
  263.4 35.1 %shard_map.189.refs_0_ = bf16[2,4,4,192,768]{4,3,2,1,0:T(8,128)(2,1)S(1)} custom-call(bf16[2,192,768]{2,1,0:T(8,128)(2,1)} %get-tuple-element.38.fresh), custom_call_target="tpu_custom_call" | custom-call | tf_op jit(solution)/shard_map/pallas_call | solution.py:420
  298.5 3.8 %shard_map.190 = bf16[2,4,4,192,768]{4,3,2,1,0:T(8,128)(2,1)} custom-call(bf16[2,4,4,192,768]{4,3,2,1,0:T(8,128)(2,1)S(1)} %shard_map.189.refs_0_), custom_call_target="tpu_custom_call" | custom-call | tf_op jit(solution)/shard_map/pallas_call | solution.py:373
